TPU v7x, 32 devices: a whole 2x2x4 slice. The times are simulated.
32 devices in a mesh: dp: 8 (over z, y), tp: 4 (over x, core).
Axes of the slice: x: 2, y: 2, z: 4, core: 2. Of those that a mesh axis runs over, the one named last changes fastest.
Arguments:
- queries: bfloat16 [64, 16, 8192], P(('dp', 'tp')), parts along dimension 0, may hold values from -512 to 512
- kv_cache: bfloat16 [64, 8, 384, 256], P(('dp', 'tp')), parts along dimension 0, may hold values from -18 to 18
- lengths: int32 [64], P(('dp', 'tp')), parts along dimension 0, may hold values from 17 to 384, as said below
- residual: bfloat16 [64, 16, 8192], P(('dp', 'tp')), parts along dimension 0, may hold values from -4 to 4
- out_weight: bfloat16 [8192, 8192], P('tp'), may hold values from -0.0625 to 0.0625
- norm_gain: bfloat16 [8192], replicated, may hold values from 0.25 to 1.75
Outputs:
- hidden: bfloat16 [64, 16, 8192], P(('dp', 'tp')), parts along dimension 0
- normed: bfloat16 [64, 16, 8192], P(('dp', 'tp')), parts along dimension 0
There are 8 independent parts, one for each index of `dp`. A program takes and returns all parts, laid end to end along the dimension named above; an argument that names none is the same for every part. Nothing has to cross between parts.
Inputs may be any that keep to these rules, and one draw needn't show every extreme that they name: `lengths`: some sequence of every part has exactly 384 live slots.
All inputs are finite; a program needn't handle non-finite values.
Results may differ from a plain program's by a relative error of at most 0.015.
Values may be sent and summed in bfloat16 or wider, within the bound.
A program may use at most 128 MiB of HBM per device.

v0:
```python
import functools
import math

import jax
import jax.numpy as jnp
from jax import lax
from jax.experimental import pallas as pl
from jax.experimental.pallas import tpu as pltpu
from jax.sharding import PartitionSpec as P

CORES = 2
COLUMNS = 512
LANES = 128


def block_kernel(
    n,
    lengths_ref,
    queries_ref,
    kv_ref,
    residual_ref,
    weight_ref,
    acc,
    scaled_ref,
    q_buf,
    kv_buf,
    res_buf,
    w_buf,
    att_send,
    att,
    keep,
    mate_send,
    mate_recv,
    cross_send,
    cross_recv,
    load_sem,
    kv_sem,
    w_sem,
    att_send_sem,
    att_recv_sem,
    mate_send_sem,
    mate_recv_sem,
    cross_send_sem,
    cross_recv_sem,
):
    chips = n // CORES
    seqs, draft, width = queries_ref.shape
    kv_heads, slots_kv, head_dim = kv_ref.shape[1], kv_ref.shape[2], kv_ref.shape[3] // 2
    heads = width // head_dim
    group = heads // kv_heads
    own_heads = heads // n
    unit_heads = min(own_heads, group)
    units = own_heads // unit_heads
    kv_per_dest = kv_buf.shape[2]
    rows = seqs * draft
    chunks, depth, columns = w_buf.shape
    model = chunks * columns

    me = lax.axis_index("tp")
    chip, core = me // CORES, me % CORES

    def device(dx, dk):
        return ((chip + dx) % chips) * CORES + (core + dk) % CORES

    def slot_of(dx, dk):
        return dx * CORES + dk

    order = [(dx, dk) for dx in range(1, chips) for dk in range(CORES)] + [(0, 1), (0, 0)]

    q_copy = pltpu.make_async_copy(queries_ref, q_buf, load_sem.at[0])
    q_copy.start()
    kv_copies = []
    for step, (dx, dk) in enumerate(order):
        first = device(dx, dk) * own_heads // group
        copy = pltpu.make_async_copy(
            kv_ref.at[:, pl.ds(first, kv_per_dest)], kv_buf.at[step], kv_sem.at[step]
        )
        copy.start()
        kv_copies.append(copy)

    def w_copy(c):
        at = pl.multiple_of(c * columns, LANES)
        return pltpu.make_async_copy(
            weight_ref.at[:, pl.ds(at, columns)], w_buf.at[c], w_sem.at[c]
        )

    def start_w(c, carry):
        w_copy(c).start()
        return carry

    lax.fori_loop(0, chunks, start_w, 0)
    res_copy = pltpu.make_async_copy(residual_ref, res_buf, load_sem.at[1])
    res_copy.start()

    barrier = pltpu.get_barrier_semaphore()
    for dx, dk in order[:-1]:
        pl.semaphore_signal(
            barrier,
            inc=1,
            device_id={"tp": device(dx, dk)},
            device_id_type=pl.DeviceIdType.MESH,
        )
    pl.semaphore_wait(barrier, n - 1)

    q_copy.wait()
    position = lax.broadcasted_iota(jnp.int32, (draft, slots_kv), 1)
    token = lax.broadcasted_iota(jnp.int32, (draft, slots_kv), 0)
    biases = [
        jnp.where(position < lengths_ref[s] - draft + 1 + token, 0.0, -1e30).astype(jnp.float32)
        for s in range(seqs)
    ]
    factor = head_dim ** (-0.5) * math.log2(math.e)

    def att_copy(dx, dk, s, source_slot, target_slot):
        part = pl.ds(s * draft, draft)
        return pltpu.make_async_remote_copy(
            src_ref=att_send.at[source_slot, part],
            dst_ref=att.at[target_slot, part],
            send_sem=att_send_sem.at[source_slot, s],
            recv_sem=att_recv_sem.at[target_slot, s],
            device_id={"tp": device(dx, dk)},
            device_id_type=pl.DeviceIdType.MESH,
        )

    for step, (dx, dk) in enumerate(order):
        slot = slot_of(dx, dk)
        dest = device(dx, dk)
        kv_copies[step].wait()
        target = att if slot == 0 else att_send
        for s in range(seqs):
            for u in range(units):
                kv_at = u if own_heads >= group else 0
                start = pl.multiple_of((dest * own_heads + u * unit_heads) * head_dim, LANES)
                wide = q_buf[s, :, pl.ds(start, unit_heads * head_dim)]
                q_rows = jnp.concatenate(
                    [wide[:, h * head_dim : (h + 1) * head_dim] for h in range(unit_heads)], axis=0
                )
                keys = kv_buf[step, s, kv_at, :, :head_dim]
                values = kv_buf[step, s, kv_at, :, head_dim:]
                scores = lax.dot_general(
                    q_rows, keys, (((1,), (1,)), ((), ())), preferred_element_type=jnp.float32
                )
                scores = scores.reshape(unit_heads, draft, slots_kv) + biases[s][None]
                peak = jnp.max(scores, axis=-1, keepdims=True)
                raised = jnp.exp2((scores - peak) * factor)
                totals = jnp.sum(raised, axis=-1, keepdims=True)
                out = jnp.dot(
                    raised.astype(jnp.bfloat16).reshape(unit_heads * draft, slots_kv),
                    values,
                    preferred_element_type=jnp.float32,
                )
                out = (out * (1.0 / totals).reshape(unit_heads * draft, 1)).astype(jnp.bfloat16)
                for h in range(unit_heads):
                    at = (u * unit_heads + h) * head_dim
                    target[slot, s * draft : (s + 1) * draft, at : at + head_dim] = out[
                        h * draft : (h + 1) * draft
                    ]
            if slot:
                att_copy(dx, dk, s, slot, slot_of((chips - dx) % chips, dk)).start()

    for dx, dk in order[:-1]:
        slot = slot_of(dx, dk)
        for s in range(seqs):
            att_copy(dx, dk, s, slot, slot).wait_recv()

    def mate_copy(c):
        return pltpu.make_async_remote_copy(
            src_ref=mate_send.at[c],
            dst_ref=mate_recv.at[c],
            send_sem=mate_send_sem.at[c],
            recv_sem=mate_recv_sem.at[c],
            device_id={"tp": device(0, 1)},
            device_id_type=pl.DeviceIdType.MESH,
        )

    def cross_copy(dx, source, target, c):
        return pltpu.make_async_remote_copy(
            src_ref=cross_send.at[source, c],
            dst_ref=cross_recv.at[target, c],
            send_sem=cross_send_sem.at[source, c],
            recv_sem=cross_recv_sem.at[target, c],
            device_id={"tp": device(dx, 0)},
            device_id_type=pl.DeviceIdType.MESH,
        )

    def multiply(c):
        w_copy(c).wait()
        product = jnp.dot(
            att[...].reshape(n * rows, depth), w_buf[c], preferred_element_type=jnp.float32
        )
        for dx in range(chips):
            own, other = slot_of(dx, 0) * rows, slot_of(dx, 1) * rows
            mate_send[c, dx] = product[other : other + rows].astype(jnp.bfloat16)
            keep[c % 2, dx] = product[own : own + rows]
        mate_copy(c).start()

    def pass_on(c):
        mate_copy(c).wait_recv()
        for dx in range(1, chips):
            both = keep[c % 2, dx] + mate_recv[c, dx].astype(jnp.float32)
            cross_send[dx - 1, c] = both.astype(jnp.bfloat16)
            cross_copy(dx, dx - 1, chips - dx - 1, c).start()
        at = pl.multiple_of(c * columns, LANES)
        own = keep[c % 2, 0] + mate_recv[c, 0].astype(jnp.float32)
        acc[:, :, pl.ds(at, columns)] = own.reshape(seqs, draft, columns)

    multiply(0)

    def both_steps(c, carry):
        multiply(c)
        pass_on(c - 1)
        return carry

    lax.fori_loop(1, chunks, both_steps, 0)
    pass_on(chunks - 1)

    res_copy.wait()

    def collect(c, squares):
        at = pl.multiple_of(c * columns, LANES)
        total = acc[:, :, pl.ds(at, columns)]
        for dx in range(1, chips):
            cross_copy(dx, dx - 1, dx - 1, c).wait_recv()
            part = cross_recv[dx - 1, c].astype(jnp.float32)
            total = total + part.reshape(seqs, draft, columns)
        total = total + res_buf[:, :, pl.ds(at, columns)].astype(jnp.float32)
        acc[:, :, pl.ds(at, columns)] = total
        for tile in range(columns // LANES):
            part = total[:, :, tile * LANES : (tile + 1) * LANES]
            squares = squares + part * part
        return squares

    squares = lax.fori_loop(0, chunks, collect, jnp.zeros((seqs, draft, LANES), jnp.float32))
    scales = lax.rsqrt(jnp.sum(squares, axis=-1, keepdims=True) / model + 1e-05)

    def scale(c, carry):
        at = pl.multiple_of(c * columns, LANES)
        scaled_ref[:, :, pl.ds(at, columns)] = acc[:, :, pl.ds(at, columns)] * scales
        return carry

    lax.fori_loop(0, chunks, scale, 0)

    for dx, dk in order[:-1]:
        slot = slot_of(dx, dk)
        for s in range(seqs):
            att_copy(dx, dk, s, slot, slot).wait_send()

    def settle(c, carry):
        mate_copy(c).wait_send()
        for dx in range(1, chips):
            cross_copy(dx, dx - 1, dx - 1, c).wait_send()
        return carry

    lax.fori_loop(0, chunks, settle, 0)


def on_device(n, queries, kv_cache, lengths, residual, out_weight, norm_gain):
    seqs, draft, width = queries.shape
    kv_heads, slots_kv, pair_dim = kv_cache.shape[1:]
    head_dim = pair_dim // 2
    heads = width // head_dim
    depth, model = out_weight.shape
    chips = n // CORES
    rows = seqs * draft
    columns = math.gcd(model, COLUMNS)
    chunks = model // columns
    kv_per_dest = max(1, kv_heads // n)
    bf16, f32 = jnp.bfloat16, jnp.float32
    dma = pltpu.SemaphoreType.DMA
    summed, scaled = pl.pallas_call(
        functools.partial(block_kernel, n),
        out_shape=(
            pltpu.VMEM(residual.shape, f32),
            pltpu.VMEM(residual.shape, f32),
        ),
        in_specs=[pl.BlockSpec(memory_space=pltpu.SMEM)]
        + [pl.BlockSpec(memory_space=pl.ANY)] * 4,
        out_specs=[pl.BlockSpec(memory_space=pltpu.VMEM)] * 2,
        scratch_shapes=[
            pltpu.VMEM(queries.shape, bf16),
            pltpu.VMEM((n, seqs, kv_per_dest, slots_kv, pair_dim), bf16),
            pltpu.VMEM(residual.shape, bf16),
            pltpu.VMEM((chunks, depth, columns), bf16),
            pltpu.VMEM((n, rows, depth), bf16),
            pltpu.VMEM((n, rows, depth), bf16),
            pltpu.VMEM((2, chips, rows, columns), f32),
            pltpu.VMEM((chunks, chips, rows, columns), bf16),
            pltpu.VMEM((chunks, chips, rows, columns), bf16),
            pltpu.VMEM((max(1, chips - 1), chunks, rows, columns), bf16),
            pltpu.VMEM((max(1, chips - 1), chunks, rows, columns), bf16),
            dma((2,)),
            dma((n,)),
            dma((chunks,)),
            dma((n, seqs)),
            dma((n, seqs)),
            dma((chunks,)),
            dma((chunks,)),
            dma((max(1, chips - 1), chunks)),
            dma((max(1, chips - 1), chunks)),
        ],
        compiler_params=pltpu.CompilerParams(
            collective_id=0, has_side_effects=True, vmem_limit_bytes=56 * 1024 * 1024
        ),
    )(lengths, queries, kv_cache, residual, out_weight)
    normed = scaled * norm_gain.astype(f32)
    return summed.astype(bf16), normed.astype(bf16)


def solution(mesh):
    return jax.shard_map(
        functools.partial(on_device, mesh.shape["tp"]),
        mesh=mesh,
        in_specs=(
            P(("dp", "tp"), None, None),
            P(("dp", "tp"), None, None, None),
            P(("dp", "tp")),
            P(("dp", "tp"), None, None),
            P("tp", None),
            P(),
        ),
        out_specs=(P(("dp", "tp"), None, None), P(("dp", "tp"), None, None)),
        check_vma=False,
    )
```

profile of v0, /device:TPU:0, one launch (start us, length us, event | category | flops | bytes accessed | tf_op | source)
XLA Modules:
  0.0 30.7 jit_solution(16768082838318897704)
XLA Ops:
  0.6 0.0 copy-start
  0.6 28.3 %shard_map.77 = (f32[2,16,8192]{2,1,0:T(8,128)S(1)}, f32[2,16,8192]{2,1,0:T(8,128)S(1)}) custom-call(s32[2]{0:T(128)} %lengths_ref.1, bf16[2,16,8192]{2,1,0:T(8,128)(2,1)} %queries_ref.1, bf16[2,8,384,256]{3,2,1,0:T(8,128)(2,1)} %kv_ref.1, bf16[2,16,8192]{2,1,0:T(8,128)(2,1)} %residual_ref.1, bf16[2048,8192]{1,0:T(8,128)(2,1)} %weight_ref.1), custom_call_target="tpu_custom_call" | custom-call | tf_op jit(solution)/shard_map/pallas_call | solution.py:270
  28.9 0.8 %convert_element_type.9 = bf16[2,16,8192]{2,1,0:T(8,128)(2,1)} convert(f32[2,16,8192]{2,1,0:T(8,128)S(1)} %get-tuple-element.4) | non-fusion elementwise | flops 262144 | bytes 1572864 | tf_op jit(solution)/shard_map/convert_element_type | solution.py:306
  29.8 0.0 copy-done
  29.8 0.9 %multiply_convert_fusion = bf16[2,16,8192]{2,1,0:T(8,128)(2,1)} fusion(f32[2,16,8192]{2,1,0:T(8,128)S(1)} %get-tuple-element.5, f32[8192]{0:T(1024)S(1)} %convert_element_type.10), kind=kLoop, calls=%fused_computation | loop fusion | flops 524288 | bytes 1605632 | tf_op jit(solution)/shard_map/convert_element_type | solution.py:306
  (1 shorter events, 0.0 us)
Async XLA Ops:
  0.6 29.2 %copy-start = (bf16[8192]{0:T(1024)(128)(2,1)S(1)}, bf16[8192]{0:T(1024)(128)(2,1)}, u32[]{:S(2)}) copy-start(bf16[8192]{0:T(1024)(128)(2,1)} %param.11) | copy-start | bytes 49156
where the time goes:
time: 30.8 us; the launch traced here: 30.7 us
  Pallas kernels  28.3 us (92%)
  other arithmetic  1.71 us (6%)
  between operations  0.65 us (2%)
    pallas_call x1, Pallas kernels, on_device(): pl.pallas_call(functools.partial(block_kernel, n), out_shape=(pltpu.VMEM(...  28.3 us
    convert_element_type x2, other arithmetic, on_device(): return (summed.astype(bf16), normed.astype(bf16))  1.71 us

commit v1 on v0

v1 whole, which is shorter than its diff:
```python
import functools
import math

import jax
import jax.numpy as jnp
from jax import lax
from jax.experimental import pallas as pl
from jax.experimental.pallas import tpu as pltpu
from jax.sharding import PartitionSpec as P

CORES = 2
COLUMNS = 1024
LANES = 128
LAG = 2
AHEAD = 5


def block_kernel(
    n,
    split,
    lengths_ref,
    queries_ref,
    kv_ref,
    residual_ref,
    weight_ref,
    gain_ref,
    acc,
    scale_ref,
    wide_gain,
    length_buf,
    gain_buf,
    q_buf,
    kv_buf,
    res_buf,
    w_buf,
    att_send,
    att,
    keep,
    mate_send,
    mate_recv,
    cross_send,
    cross_recv,
    small_sem,
    q_sem,
    kv_sem,
    w_sem,
    att_send_sem,
    att_recv_sem,
    mate_send_sem,
    mate_recv_sem,
    cross_send_sem,
    cross_recv_sem,
):
    chips = n // CORES
    seqs, draft, width = queries_ref.shape
    kv_heads, slots_kv, head_dim = kv_ref.shape[1], kv_ref.shape[2], kv_ref.shape[3] // 2
    heads = width // head_dim
    group = heads // kv_heads
    own_heads = heads // n
    unit_heads = min(own_heads, group)
    units = own_heads // unit_heads
    kv_per_dest = kv_buf.shape[1]
    rows = seqs * draft
    chunks, depth, columns = w_buf.shape
    model = chunks * columns

    early = seqs // 2
    late = seqs - early
    early_rows, late_rows = early * draft, late * draft
    others = chips - 1
    local_at = others * CORES * early_rows
    late_at = local_at + CORES * rows
    att_rows = late_at + others * CORES * late_rows
    mate_local = others * early_rows
    mate_late = mate_local + rows
    mate_rows = mate_late + others * late_rows

    me = lax.axis_index("tp")
    chip, core = me // CORES, me % CORES

    def device(dx, dk):
        return ((chip + dx) % chips) * CORES + (core + dk) % CORES

    def att_row(dx, dk, s):
        if dx == 0:
            return local_at + dk * rows + s * draft
        place = (dx - 1) * CORES + dk
        if s < early:
            return place * early_rows + s * draft
        return late_at + place * late_rows + (s - early) * draft

    remote = [(dx, dk) for dx in range(1, chips) for dk in range(CORES)]
    order = [(dx, dk, s) for s in range(seqs) for dx, dk in remote]
    order += [(0, 1, s) for s in range(seqs)] + [(0, 0, s) for s in range(seqs)]

    barrier = pltpu.get_barrier_semaphore()
    for dx, dk in [(0, 1)] + remote:
        pl.semaphore_signal(
            barrier,
            inc=1,
            device_id={"tp": device(dx, dk)},
            device_id_type=pl.DeviceIdType.MESH,
        )

    def q_copy(s):
        return pltpu.make_async_copy(queries_ref.at[s], q_buf.at[s], q_sem.at[s])

    def kv_copy(step):
        dx, dk, s = order[step]
        first = device(dx, dk) * own_heads // group
        return pltpu.make_async_copy(
            kv_ref.at[s, pl.ds(first, kv_per_dest)], kv_buf.at[step], kv_sem.at[step]
        )

    length_copy = pltpu.make_async_copy(lengths_ref, length_buf, small_sem.at[0])
    gain_copy = pltpu.make_async_copy(gain_ref, gain_buf, small_sem.at[1])
    res_copy = pltpu.make_async_copy(residual_ref, res_buf, small_sem.at[2])
    length_copy.start()
    seen = set()
    for step, (_, _, s) in enumerate(order):
        if s not in seen:
            seen.add(s)
            q_copy(s).start()
        kv_copy(step).start()

    def w_copy(c):
        at = pl.multiple_of(c * columns, LANES)
        return pltpu.make_async_copy(
            weight_ref.at[:, pl.ds(at, columns)], w_buf.at[c], w_sem.at[c]
        )

    length_copy.wait()
    position = lax.broadcasted_iota(jnp.int32, (draft, slots_kv), 1)
    token = lax.broadcasted_iota(jnp.int32, (draft, slots_kv), 0)
    biases = [
        jnp.where(position < length_buf[s] - draft + 1 + token, 0.0, -1e30).astype(jnp.float32)
        for s in range(seqs)
    ]
    factor = head_dim ** (-0.5) * math.log2(math.e)

    def attend(step, u):
        dx, dk, s = order[step]
        kv_at = u if own_heads >= group else 0
        dest = device(dx, dk)
        start = pl.multiple_of((dest * own_heads + u * unit_heads) * head_dim, LANES)
        wide = q_buf[s, :, pl.ds(start, unit_heads * head_dim)]
        q_rows = jnp.concatenate(
            [wide[:, h * head_dim : (h + 1) * head_dim] for h in range(unit_heads)], axis=0
        )
        keys = kv_buf[step, kv_at, :, :head_dim]
        values = kv_buf[step, kv_at, :, head_dim:]
        scores = lax.dot_general(
            q_rows, keys, (((1,), (1,)), ((), ())), preferred_element_type=jnp.float32
        )
        scores = scores.reshape(unit_heads, draft, slots_kv) + biases[s][None]
        peak = jnp.max(scores, axis=-1, keepdims=True)
        raised = jnp.exp2((scores - peak) * factor)
        totals = jnp.sum(raised, axis=-1, keepdims=True)
        out = jnp.dot(
            raised.astype(jnp.bfloat16).reshape(unit_heads * draft, slots_kv),
            values,
            preferred_element_type=jnp.float32,
        )
        return (out * (1.0 / totals).reshape(unit_heads * draft, 1)).astype(jnp.bfloat16)

    def att_copy(dx, dk, s):
        slot = dx * CORES + dk - 1
        if dx == 0:
            recv = 2
        else:
            recv = 0 if s < early else 1
        return pltpu.make_async_remote_copy(
            src_ref=att_send.at[slot, pl.ds(s * draft, draft)],
            dst_ref=att.at[pl.ds(att_row((chips - dx) % chips, dk, s), draft)],
            send_sem=att_send_sem,
            recv_sem=att_recv_sem.at[recv],
            device_id={"tp": device(dx, dk)},
            device_id_type=pl.DeviceIdType.MESH,
        )

    ahead = max(1, chunks * AHEAD // 8) if split else chunks
    waited = set()
    for step, (dx, dk, s) in enumerate(order):
        slot = dx * CORES + dk
        if s not in waited:
            waited.add(s)
            q_copy(s).wait()
        kv_copy(step).wait()
        for c in range(ahead * step // len(order), ahead * (step + 1) // len(order)):
            w_copy(c).start()
        for u in range(units):
            out = attend(step, u)
            for h in range(unit_heads):
                at = (u * unit_heads + h) * head_dim
                piece = out[h * draft : (h + 1) * draft]
                if slot:
                    att_send[slot - 1, s * draft : (s + 1) * draft, at : at + head_dim] = piece
                else:
                    own = att_row(0, 0, s)
                    att[own : own + draft, at : at + head_dim] = piece
        if step == 0:
            pl.semaphore_wait(barrier, n - 1)
        if slot:
            att_copy(dx, dk, s).start()

    def att_arrived(first, count, which):
        block = att.at[pl.ds(first, count)]
        pltpu.make_async_copy(block, block, att_recv_sem.at[which]).wait()

    def mate_copy(first, count, c, which):
        part = pl.ds(first, count)
        return pltpu.make_async_remote_copy(
            src_ref=mate_send.at[c, part],
            dst_ref=mate_recv.at[c, part],
            send_sem=mate_send_sem,
            recv_sem=mate_recv_sem.at[which],
            device_id={"tp": device(0, 1)},
            device_id_type=pl.DeviceIdType.MESH,
        )

    def cross_copy(dx, first, count, c, which):
        part = pl.ds(first, count)
        return pltpu.make_async_remote_copy(
            src_ref=cross_send.at[dx - 1, c, part],
            dst_ref=cross_recv.at[chips - dx - 1, c, part],
            send_sem=cross_send_sem,
            recv_sem=cross_recv_sem.at[which],
            device_id={"tp": device(dx, 0)},
            device_id_type=pl.DeviceIdType.MESH,
        )

    FIRST, REST, ALL = 0, 1, 2
    att_span = {FIRST: (0, late_at), REST: (late_at, att_rows), ALL: (0, att_rows)}
    mate_span = {FIRST: (0, mate_late), REST: (mate_late, mate_rows), ALL: (0, mate_rows)}
    cross_span = {FIRST: (0, early_rows), REST: (early_rows, rows), ALL: (0, rows)}

    def mate_slot(kind, c):
        return c if kind == FIRST else split + c

    def cross_slot(kind, c):
        return 0 if kind == FIRST else 1 + c

    def mate_item(kind, c):
        low, high = mate_span[kind]
        return mate_copy(low, high - low, c, mate_slot(kind, c))

    def multiply(kind, c):
        low, high = att_span[kind]
        product = jnp.dot(att[low:high], w_buf[c], preferred_element_type=jnp.float32)

        def part(first, count):
            return product[first - low : first - low + count]

        for dx in range(1, chips):
            if kind != REST and early:
                at = att_row(dx, 0, 0)
                keep[c, dx - 1, 0:early_rows] = part(at, early_rows)
                to = (dx - 1) * early_rows
                mate_send[c, to : to + early_rows] = part(at + early_rows, early_rows).astype(
                    jnp.bfloat16
                )
            if kind != FIRST:
                at = att_row(dx, 0, early)
                keep[c, dx - 1, early_rows:rows] = part(at, late_rows)
                to = mate_late + (dx - 1) * late_rows
                mate_send[c, to : to + late_rows] = part(at + late_rows, late_rows).astype(
                    jnp.bfloat16
                )
        if kind != REST:
            at = pl.multiple_of(c * columns, LANES)
            acc[:, :, pl.ds(at, columns)] = part(local_at, rows).reshape(seqs, draft, columns)
            mate_send[c, mate_local:mate_late] = part(local_at + rows, rows).astype(jnp.bfloat16)
        mate_item(kind, c).start()

    def pass_on(kind, c):
        mate_item(kind, c).wait_recv()
        low, high = cross_span[kind]
        for dx in range(1, chips):
            if kind != REST and early:
                at = (dx - 1) * early_rows
                both = keep[c, dx - 1, 0:early_rows] + mate_recv[c, at : at + early_rows].astype(
                    jnp.float32
                )
                cross_send[dx - 1, c, 0:early_rows] = both.astype(jnp.bfloat16)
            if kind != FIRST:
                at = mate_late + (dx - 1) * late_rows
                both = keep[c, dx - 1, early_rows:rows] + mate_recv[
                    c, at : at + late_rows
                ].astype(jnp.float32)
                cross_send[dx - 1, c, early_rows:rows] = both.astype(jnp.bfloat16)
            cross_copy(dx, low, high - low, c, cross_slot(kind, c)).start()
        if kind != REST:
            at = pl.multiple_of(c * columns, LANES)
            other = mate_recv[c, mate_local:mate_late].astype(jnp.float32)
            residual = res_buf[:, :, pl.ds(at, columns)].astype(jnp.float32)
            acc[:, :, pl.ds(at, columns)] += other.reshape(seqs, draft, columns) + residual

    def sweep(kind, first, last, before, wait_w):
        lag = min(LAG, last - first)

        def step(c, carry):
            if wait_w:
                w_copy(c).wait()
            if kind == FIRST:

                @pl.when(c + ahead < chunks)
                def _():
                    w_copy(c + ahead).start()

            multiply(kind, c)
            if before is not None:
                kind_before, last_before, lag_before = before

                @pl.when(c - first < lag_before)
                def _():
                    pass_on(kind_before, last_before - lag_before + c - first)

            @pl.when(c - first >= lag)
            def _():
                pass_on(kind, c - lag)

            return carry

        lax.fori_loop(first, last, step, 0)
        done = 0 if before is None else min(before[2], last - first)
        if before is not None:
            for c in range(before[1] - before[2] + done, before[1]):
                pass_on(before[0], c)
        return kind, last, lag

    res_copy.start()
    gain_copy.start()
    before = None
    att_arrived(local_at + rows, rows, 2)
    if early:
        att_arrived(0, local_at, 0)
    res_copy.wait()
    if split:
        before = sweep(FIRST, 0, split, None, True)
    att_arrived(late_at, att_rows - late_at, 1)
    if split < chunks:
        before = sweep(ALL, split, chunks, before, True)
    if split:
        before = sweep(REST, 0, split, before, False)
    for c in range(before[1] - before[2], before[1]):
        pass_on(before[0], c)

    def arrived(kind, c, count):
        low, high = cross_span[kind]
        block = cross_recv.at[:, pl.ds(c, count), pl.ds(low, high - low)]
        pltpu.make_async_copy(block, block, cross_recv_sem.at[cross_slot(kind, c)]).wait()

    def collect(kind, c, squares):
        low, high = cross_span[kind]
        at = pl.multiple_of(c * columns, LANES)
        s0, s1 = low // draft, high // draft
        total = acc[s0:s1, :, pl.ds(at, columns)]
        for dx in range(1, chips):
            part = cross_recv[dx - 1, c, low:high].astype(jnp.float32)
            total = total + part.reshape(s1 - s0, draft, columns)
        acc[s0:s1, :, pl.ds(at, columns)] = total
        for tile in range(columns // LANES):
            part = total[:, :, tile * LANES : (tile + 1) * LANES]
            squares = squares + part * part
        return squares

    gain_copy.wait()
    wide_gain[...] = gain_buf[...].astype(jnp.float32)

    def finish(kind, c, squares):
        arrived(kind, c, 1)
        return collect(kind, c, squares)

    def gather(kind, first, last, squares):
        return lax.fori_loop(first, last, functools.partial(finish, kind), squares)

    squares = jnp.zeros((seqs, draft, LANES), jnp.float32)
    if split:
        arrived(FIRST, 0, split)
        first = lax.fori_loop(0, split, functools.partial(collect, FIRST), squares[:early])
    squares = gather(ALL, split, chunks, squares)
    if split:
        last = gather(REST, 0, split, squares[early:])
        squares = jnp.concatenate([first + squares[:early], last], axis=0)
    mean = jnp.sum(squares, axis=-1, keepdims=True) / model
    scale_ref[...] = jnp.broadcast_to(lax.rsqrt(mean + 1e-05), scale_ref.shape)

    pltpu.make_async_copy(att_send, att_send, att_send_sem).wait()
    pltpu.make_async_copy(mate_send, mate_send, mate_send_sem).wait()
    pltpu.make_async_copy(cross_send, cross_send, cross_send_sem).wait()


def on_device(n, queries, kv_cache, lengths, residual, out_weight, norm_gain):
    seqs, draft, width = queries.shape
    kv_heads, slots_kv, pair_dim = kv_cache.shape[1:]
    head_dim = pair_dim // 2
    heads = width // head_dim
    depth, model = out_weight.shape
    chips = n // CORES
    others = max(1, chips - 1)
    rows = seqs * draft
    columns = math.gcd(model, COLUMNS)
    chunks = model // columns
    split = chunks // 2 if seqs > 1 and chips > 1 else 0
    kv_per_dest = max(1, kv_heads // n)
    bf16, f32 = jnp.bfloat16, jnp.float32
    dma = pltpu.SemaphoreType.DMA
    summed, scale, gain = pl.pallas_call(
        functools.partial(block_kernel, n, split),
        out_shape=(
            pltpu.VMEM(residual.shape, f32),
            pltpu.VMEM((seqs, draft, LANES), f32),
            pltpu.VMEM(norm_gain.shape, f32),
        ),
        in_specs=[pl.BlockSpec(memory_space=pl.ANY)] * 6,
        out_specs=[pl.BlockSpec(memory_space=pltpu.VMEM)] * 3,
        scratch_shapes=[
            pltpu.SMEM(lengths.shape, jnp.int32),
            pltpu.VMEM(norm_gain.shape, bf16),
            pltpu.VMEM(queries.shape, bf16),
            pltpu.VMEM((n * seqs, kv_per_dest, slots_kv, pair_dim), bf16),
            pltpu.VMEM(residual.shape, bf16),
            pltpu.VMEM((chunks, depth, columns), bf16),
            pltpu.VMEM((n - 1, rows, depth), bf16),
            pltpu.VMEM((n * rows, depth), bf16),
            pltpu.VMEM((chunks, others, rows, columns), f32),
            pltpu.VMEM((chunks, chips * rows, columns), bf16),
            pltpu.VMEM((chunks, chips * rows, columns), bf16),
            pltpu.VMEM((others, chunks, rows, columns), bf16),
            pltpu.VMEM((others, chunks, rows, columns), bf16),
            dma((3,)),
            dma((seqs,)),
            dma((n * seqs,)),
            dma((chunks,)),
            dma,
            dma((3,)),
            dma,
            dma((chunks + split,)),
            dma,
            dma((1 + chunks,)),
        ],
        compiler_params=pltpu.CompilerParams(
            collective_id=0, has_side_effects=True, vmem_limit_bytes=56 * 1024 * 1024
        ),
    )(lengths, queries, kv_cache, residual, out_weight, norm_gain)
    normed = summed * scale[:, :, :1] * gain
    return summed.astype(bf16), normed.astype(bf16)


def solution(mesh):
    return jax.shard_map(
        functools.partial(on_device, mesh.shape["tp"]),
        mesh=mesh,
        in_specs=(
            P(("dp", "tp"), None, None),
            P(("dp", "tp"), None, None, None),
            P(("dp", "tp")),
            P(("dp", "tp"), None, None),
            P("tp", None),
            P(),
        ),
        out_specs=(P(("dp", "tp"), None, None), P(("dp", "tp"), None, None)),
        check_vma=False,
    )
```

time: 30.8 us -> 28.9 us (0.938)
  Pallas kernels: 28.3 us -> 26.9 us
  other arithmetic: 1.71 us -> 1.14 us
    pallas_call x1, Pallas kernels: 28.3 us -> 26.9 us  [on_device(): pl.pallas_call(functools.partial(block_kernel, n, split), out_shape=(pltp...]
    convert_element_type x2 -> x1, other arithmetic: 1.71 us -> 1.14 us  [on_device(): return (summed.astype(bf16), normed.astype(bf16))]
where the time goes in v1:
time: 28.9 us; the launch traced here: 28.8 us
  Pallas kernels  26.9 us (93%)
  other arithmetic  1.14 us (4%)
  between operations  0.64 us (2%)
    pallas_call x1, Pallas kernels, on_device(): pl.pallas_call(functools.partial(block_kernel, n, split), out_shape=(pltp...  26.9 us
    convert_element_type x1, other arithmetic, on_device(): return (summed.astype(bf16), normed.astype(bf16))  1.14 us

profile of v1, /device:TPU:0, one launch (start us, length us, event | category | flops | bytes accessed | tf_op | source)
XLA Modules:
  0.0 28.8 jit_solution(10429315308445562749)
XLA Ops:
  0.6 26.9 %shard_map.77 = (f32[2,16,8192]{2,1,0:T(8,128)S(1)}, f32[2,16,128]{2,1,0:T(8,128)S(1)}, f32[8192]{0:T(1024)S(1)}) custom-call(s32[2]{0:T(128)} %lengths_ref.1, bf16[2,16,8192]{2,1,0:T(8,128)(2,1)} %queries_ref.1, bf16[2,8,384,256]{3,2,1,0:T(8,128)(2,1)} %kv_ref.1, bf16[2,16,8192]{2,1,0:T(8,128)(2,1)} %residual_ref.1, bf16[2048,8192]{1,0:T(8,128)(2,1)} %weight_ref.1, ...), custom_call_target="tpu_custom_call" | custom-call | tf_op jit(solution)/shard_map/pallas_call | solution.py:408
  27.5 0.1 slice_reduce_fusion
  27.6 1.1 %multiply_convert_fusion = (bf16[2,16,8192]{2,1,0:T(8,128)(2,1)}, bf16[2,16,8192]{2,1,0:T(8,128)(2,1)}) fusion(f32[2,16,8192]{2,1,0:T(8,128)S(1)} %get-tuple-element.5, f32[8192]{0:T(1024)S(1)} %get-tuple-element.7, f32[2,16]{1,0:T(2,128)S(1)} %slice_reduce_fusion), kind=kLoop, calls=%fused_computation | loop fusion | flops 1048576 | bytes 2130048 | tf_op jit(solution)/shard_map/convert_element_type | solution.py:447

commit v2 on v1

--- a/solution.py
+++ b/solution.py
@@ -12,7 +12,6 @@
 COLUMNS = 1024
 LANES = 128
 LAG = 2
-AHEAD = 5
 
 
 def block_kernel(
@@ -138,7 +137,7 @@
     ]
     factor = head_dim ** (-0.5) * math.log2(math.e)
 
-    def attend(step, u):
+    def score(step, u):
         dx, dk, s = order[step]
         kv_at = u if own_heads >= group else 0
         dest = device(dx, dk)
@@ -148,20 +147,27 @@
             [wide[:, h * head_dim : (h + 1) * head_dim] for h in range(unit_heads)], axis=0
         )
         keys = kv_buf[step, kv_at, :, :head_dim]
-        values = kv_buf[step, kv_at, :, head_dim:]
         scores = lax.dot_general(
             q_rows, keys, (((1,), (1,)), ((), ())), preferred_element_type=jnp.float32
         )
-        scores = scores.reshape(unit_heads, draft, slots_kv) + biases[s][None]
+        return scores.reshape(unit_heads, draft, slots_kv) + biases[s][None]
+
+    def weigh(scores):
         peak = jnp.max(scores, axis=-1, keepdims=True)
         raised = jnp.exp2((scores - peak) * factor)
-        totals = jnp.sum(raised, axis=-1, keepdims=True)
-        out = jnp.dot(
-            raised.astype(jnp.bfloat16).reshape(unit_heads * draft, slots_kv),
-            values,
-            preferred_element_type=jnp.float32,
-        )
-        return (out * (1.0 / totals).reshape(unit_heads * draft, 1)).astype(jnp.bfloat16)
+        return raised.astype(jnp.bfloat16).reshape(unit_heads * draft, slots_kv)
+
+    def mix(step, u, weights):
+        kv_at = u if own_heads >= group else 0
+        values = kv_buf[step, kv_at, :, head_dim:]
+        both = jnp.concatenate([values, jnp.ones_like(values)], axis=1)
+        out = jnp.dot(weights, both, preferred_element_type=jnp.float32)
+        return (out[:, :head_dim] / out[:, head_dim:]).astype(jnp.bfloat16)
+
+    def attend_all(items):
+        scores = [score(*item) for item in items]
+        weights = [weigh(x) for x in scores]
+        return [(item, mix(*item, x)) for item, x in zip(items, weights)]
 
     def att_copy(dx, dk, s):
         slot = dx * CORES + dk - 1
@@ -178,18 +184,24 @@
             device_id_type=pl.DeviceIdType.MESH,
         )
 
-    ahead = max(1, chunks * AHEAD // 8) if split else chunks
+    for c in range(split or chunks):
+        w_copy(c).start()
+    far = sum(1 for dx, _, _ in order if dx)
+    blocks = [[step] for step in range(min(2, far))]
+    blocks += [list(range(step, min(step + 2, far))) for step in range(2, far, 2)]
+    blocks.append(list(range(far, len(order))))
     waited = set()
-    for step, (dx, dk, s) in enumerate(order):
-        slot = dx * CORES + dk
-        if s not in waited:
-            waited.add(s)
-            q_copy(s).wait()
-        kv_copy(step).wait()
-        for c in range(ahead * step // len(order), ahead * (step + 1) // len(order)):
-            w_copy(c).start()
-        for u in range(units):
-            out = attend(step, u)
+    for block in blocks:
+        for step in block:
+            s = order[step][2]
+            if s not in waited:
+                waited.add(s)
+                q_copy(s).wait()
+            kv_copy(step).wait()
+        done = attend_all([(step, u) for step in block for u in range(units)])
+        for (step, u), out in done:
+            dx, dk, s = order[step]
+            slot = dx * CORES + dk
             for h in range(unit_heads):
                 at = (u * unit_heads + h) * head_dim
                 piece = out[h * draft : (h + 1) * draft]
@@ -198,10 +210,11 @@
                 else:
                     own = att_row(0, 0, s)
                     att[own : own + draft, at : at + head_dim] = piece
-        if step == 0:
+        if 0 in block:
             pl.semaphore_wait(barrier, n - 1)
-        if slot:
-            att_copy(dx, dk, s).start()
+        for step in block:
+            if order[step][0] or order[step][1]:
+                att_copy(*order[step]).start()
 
     def att_arrived(first, count, which):
         block = att.at[pl.ds(first, count)]
@@ -295,55 +308,56 @@
             residual = res_buf[:, :, pl.ds(at, columns)].astype(jnp.float32)
             acc[:, :, pl.ds(at, columns)] += other.reshape(seqs, draft, columns) + residual
 
-    def sweep(kind, first, last, before, wait_w):
-        lag = min(LAG, last - first)
-
-        def step(c, carry):
-            if wait_w:
-                w_copy(c).wait()
-            if kind == FIRST:
-
-                @pl.when(c + ahead < chunks)
-                def _():
-                    w_copy(c + ahead).start()
-
-            multiply(kind, c)
-            if before is not None:
-                kind_before, last_before, lag_before = before
-
-                @pl.when(c - first < lag_before)
-                def _():
-                    pass_on(kind_before, last_before - lag_before + c - first)
-
-            @pl.when(c - first >= lag)
-            def _():
-                pass_on(kind, c - lag)
-
-            return carry
-
-        lax.fori_loop(first, last, step, 0)
-        done = 0 if before is None else min(before[2], last - first)
-        if before is not None:
-            for c in range(before[1] - before[2] + done, before[1]):
-                pass_on(before[0], c)
-        return kind, last, lag
-
     res_copy.start()
     gain_copy.start()
-    before = None
     att_arrived(local_at + rows, rows, 2)
     if early:
         att_arrived(0, local_at, 0)
     res_copy.wait()
-    if split:
-        before = sweep(FIRST, 0, split, None, True)
-    att_arrived(late_at, att_rows - late_at, 1)
-    if split < chunks:
-        before = sweep(ALL, split, chunks, before, True)
-    if split:
-        before = sweep(REST, 0, split, before, False)
-    for c in range(before[1] - before[2], before[1]):
-        pass_on(before[0], c)
+
+    def sweep(kind, first, last, pending, wait_late):
+        lag = min(LAG, last - first)
+
+        def step(c, carry):
+            for k, (kind_before, c_before) in enumerate(pending):
+
+                @pl.when(c - first == k)
+                def _():
+                    pass_on(kind_before, c_before)
+
+            @pl.when(c - first >= lag)
+            def _():
+                pass_on(kind, c - lag)
+
+            if wait_late:
+
+                @pl.when(c == first)
+                def _():
+                    att_arrived(late_at, att_rows - late_at, 1)
+
+            if kind != REST:
+                w_copy(c).wait()
+                if split:
+                    later = split + c - jnp.minimum(c, 1)
+
+                    @pl.when((c != 1) & (later < chunks))
+                    def _():
+                        w_copy(later).start()
+
+            multiply(kind, c)
+            return carry
+
+        lax.fori_loop(first, last, step, 0)
+        return [(kind, c) for c in range(last - lag, last)]
+
+    sweeps = [(FIRST, 0, split), (ALL, split, chunks), (REST, 0, split)]
+    sweeps = [x for x in sweeps if x[1] < x[2]]
+    pending = []
+    for index, (kind, low, high) in enumerate(sweeps):
+        late_now = kind != FIRST and all(x[0] == FIRST for x in sweeps[:index])
+        pending = sweep(kind, low, high, pending, late_now)
+    for kind, c in pending:
+        pass_on(kind, c)
 
     def arrived(kind, c, count):
         low, high = cross_span[kind]
@@ -371,17 +385,19 @@
         arrived(kind, c, 1)
         return collect(kind, c, squares)
 
-    def gather(kind, first, last, squares):
-        return lax.fori_loop(first, last, functools.partial(finish, kind), squares)
-
-    squares = jnp.zeros((seqs, draft, LANES), jnp.float32)
+    sums = {
+        FIRST: jnp.zeros((early, draft, LANES), jnp.float32) if early else None,
+        REST: jnp.zeros((late, draft, LANES), jnp.float32),
+        ALL: jnp.zeros((seqs, draft, LANES), jnp.float32),
+    }
+    for kind, low, high in sweeps:
+        if kind == FIRST:
+            arrived(FIRST, 0, split)
+        do = collect if kind == FIRST else finish
+        sums[kind] = lax.fori_loop(low, high, functools.partial(do, kind), sums[kind])
+    squares = sums[ALL]
     if split:
-        arrived(FIRST, 0, split)
-        first = lax.fori_loop(0, split, functools.partial(collect, FIRST), squares[:early])
-    squares = gather(ALL, split, chunks, squares)
-    if split:
-        last = gather(REST, 0, split, squares[early:])
-        squares = jnp.concatenate([first + squares[:early], last], axis=0)
+        squares = squares + jnp.concatenate([sums[FIRST], sums[REST]], axis=0)
     mean = jnp.sum(squares, axis=-1, keepdims=True) / model
     scale_ref[...] = jnp.broadcast_to(lax.rsqrt(mean + 1e-05), scale_ref.shape)
 
@@ -401,7 +417,7 @@
     rows = seqs * draft
     columns = math.gcd(model, COLUMNS)
     chunks = model // columns
-    split = chunks // 2 if seqs > 1 and chips > 1 else 0
+    split = chunks // 2 if seqs > 1 and chips > 1 and chunks % 2 == 0 else 0
     kv_per_dest = max(1, kv_heads // n)
     bf16, f32 = jnp.bfloat16, jnp.float32
     dma = pltpu.SemaphoreType.DMA

time: 28.9 us -> 27.9 us (0.965)
  Pallas kernels: 26.9 us -> 25.9 us
    pallas_call x1, Pallas kernels: 26.9 us -> 25.9 us  [on_device(): pl.pallas_call(functools.partial(block_kernel, n, split), out_shape=(pltp...]
where the time goes in v2:
time: 27.9 us; the launch traced here: 27.7 us
  Pallas kernels  25.9 us (93%)
  other arithmetic  1.14 us (4%)
  between operations  0.64 us (2%)
    pallas_call x1, Pallas kernels, on_device(): pl.pallas_call(functools.partial(block_kernel, n, split), out_shape=(pltp...  25.9 us
    convert_element_type x1, other arithmetic, on_device(): return (summed.astype(bf16), normed.astype(bf16))  1.14 us

profile of v2, /device:TPU:0, one launch (start us, length us, event | category | flops | bytes accessed | tf_op | source)
XLA Modules:
  0.0 27.7 jit_solution(12283608955168131528)
XLA Ops:
  0.6 25.9 %shard_map.77 = (f32[2,16,8192]{2,1,0:T(8,128)S(1)}, f32[2,16,128]{2,1,0:T(8,128)S(1)}, f32[8192]{0:T(1024)S(1)}) custom-call(s32[2]{0:T(128)} %lengths_ref.1, bf16[2,16,8192]{2,1,0:T(8,128)(2,1)} %queries_ref.1, bf16[2,8,384,256]{3,2,1,0:T(8,128)(2,1)} %kv_ref.1, bf16[2,16,8192]{2,1,0:T(8,128)(2,1)} %residual_ref.1, bf16[2048,8192]{1,0:T(8,128)(2,1)} %weight_ref.1, ...), custom_call_target="tpu_custom_call" | custom-call | tf_op jit(solution)/shard_map/pallas_call | solution.py:424
  26.5 0.1 slice_reduce_fusion
  26.6 1.1 %multiply_convert_fusion = (bf16[2,16,8192]{2,1,0:T(8,128)(2,1)}, bf16[2,16,8192]{2,1,0:T(8,128)(2,1)}) fusion(f32[2,16,8192]{2,1,0:T(8,128)S(1)} %get-tuple-element.5, f32[8192]{0:T(1024)S(1)} %get-tuple-element.7, f32[2,16]{1,0:T(2,128)S(1)} %slice_reduce_fusion), kind=kLoop, calls=%fused_computation | loop fusion | flops 1048576 | bytes 2130048 | tf_op jit(solution)/shard_map/convert_element_type | solution.py:463

commit v3 on v2

--- a/solution.py
+++ b/solution.py
@@ -417,7 +417,7 @@
     rows = seqs * draft
     columns = math.gcd(model, COLUMNS)
     chunks = model // columns
-    split = chunks // 2 if seqs > 1 and chips > 1 and chunks % 2 == 0 else 0
+    split = chunks * 3 // 8 if seqs > 1 and chips > 1 and chunks % 2 == 0 else 0
     kv_per_dest = max(1, kv_heads // n)
     bf16, f32 = jnp.bfloat16, jnp.float32
     dma = pltpu.SemaphoreType.DMA

time: 27.9 us -> 26.7 us (0.957)
  Pallas kernels: 25.9 us -> 24.6 us
    pallas_call x1, Pallas kernels: 25.9 us -> 24.6 us  [on_device(): pl.pallas_call(functools.partial(block_kernel, n, split), out_shape=(pltp...]
where the time goes in v3:
time: 26.7 us; the launch traced here: 26.5 us
  Pallas kernels  24.6 us (92%)
  other arithmetic  1.14 us (4%)
  between operations  0.64 us (2%)
    pallas_call x1, Pallas kernels, on_device(): pl.pallas_call(functools.partial(block_kernel, n, split), out_shape=(pltp...  24.6 us
    convert_element_type x1, other arithmetic, on_device(): return (summed.astype(bf16), normed.astype(bf16))  1.14 us

profile of v3, /device:TPU:0, one launch (start us, length us, event | category | flops | bytes accessed | tf_op | source)
XLA Modules:
  0.0 26.5 jit_solution(3790508131634608762)
XLA Ops:
  0.6 24.6 %shard_map.77 = (f32[2,16,8192]{2,1,0:T(8,128)S(1)}, f32[2,16,128]{2,1,0:T(8,128)S(1)}, f32[8192]{0:T(1024)S(1)}) custom-call(s32[2]{0:T(128)} %lengths_ref.1, bf16[2,16,8192]{2,1,0:T(8,128)(2,1)} %queries_ref.1, bf16[2,8,384,256]{3,2,1,0:T(8,128)(2,1)} %kv_ref.1, bf16[2,16,8192]{2,1,0:T(8,128)(2,1)} %residual_ref.1, bf16[2048,8192]{1,0:T(8,128)(2,1)} %weight_ref.1, ...), custom_call_target="tpu_custom_call" | custom-call | tf_op jit(solution)/shard_map/pallas_call | solution.py:424
  25.3 0.1 slice_reduce_fusion
  25.4 1.1 %multiply_convert_fusion = (bf16[2,16,8192]{2,1,0:T(8,128)(2,1)}, bf16[2,16,8192]{2,1,0:T(8,128)(2,1)}) fusion(f32[2,16,8192]{2,1,0:T(8,128)S(1)} %get-tuple-element.5, f32[8192]{0:T(1024)S(1)} %get-tuple-element.7, f32[2,16]{1,0:T(2,128)S(1)} %slice_reduce_fusion), kind=kLoop, calls=%fused_computation | loop fusion | flops 1048576 | bytes 2130048 | tf_op jit(solution)/shard_map/convert_element_type | solution.py:463
